TPU v7x, 512 devices: a whole 4x8x8 slice. The times are simulated.
512 devices in a mesh: blk: 64 (over y, x, z_lo), ga: 8 (over z_hi, core).
Axes of the slice: x: 4, y: 8, z: 8 (z_hi: 4, z_lo: 2; z = z_hi * 2 + z_lo), core: 2. Of those that a mesh axis runs over, the one named last changes fastest.
Arguments:
- pair_elements: bfloat16 [4096, 65536], P('ga', 'blk'), may hold values from -6 to 6
- screening: bfloat16 [4096, 4096], P('ga', 'blk'), may hold values from -0.09375 to 0.09375
- energies: float32 [1024], replicated, may hold values from 0.5 to 3
- frequencies: float32 [8], replicated, may hold values from 0.3 to 3
- qp_index: int32 [32], replicated, may hold values from 0 to 1023
- occupied: int32 [1024], replicated, may hold values 0 or 1
Outputs:
- self_energy: float32 [2, 8, 32, 32], replicated
All inputs are finite; a program needn't handle non-finite values.
Results may differ from a plain program's by a relative error of at most 0.0003.
Values may be sent and summed in bfloat16 or wider, within the bound.
A program may use at most 64 MiB of HBM per device.

v0:
```python
import jax
import jax.numpy as jnp
from jax import lax
from jax.sharding import Mesh
from jax.sharding import PartitionSpec as P

STATES = 32
NG = 4096
BLK = ("blk_0", "blk_1", "blk_2")
BLK_GA = ("blk_0", "blk_1", "blk_2", "ga")


def laid_out(pieces, dim):
    dims = list(pieces.shape[1:])
    dims[dim] *= pieces.shape[0]
    return jnp.moveaxis(pieces, 0, dim).reshape(dims)


def all_blocks(shard, axes, order):
    pieces = shard[None]
    for k in order:
        pieces = lax.all_gather(pieces, axes[k], axis=0, tiled=True)
    block = [lax.axis_size(axes[k]) for k in reversed(order)]
    pieces = pieces.reshape(*block, *shard.shape)
    turned = sorted(range(len(order)), key=lambda place: order[len(order) - 1 - place])
    return pieces.transpose(*turned, *range(len(order), pieces.ndim)).reshape(-1, *shard.shape)


def gathered_by_axis(shard, axes, order, dim):
    return laid_out(all_blocks(shard, axes, order), dim)


def band_weights(energies, frequencies, qp_index, occupied, offset, band_count):
    level_count = energies.shape[0]
    position = jnp.arange(level_count, dtype=jnp.int32)
    signed = jnp.where(occupied == 1, -energies, energies)
    onehot = (qp_index[:, None] == position[None, :]).astype(jnp.float32)
    state_level = jnp.sum(onehot * signed[None, :], axis=1)
    band_level = lax.dynamic_slice_in_dim(signed, offset, band_count, 0)
    detuning = state_level[:, None] - band_level[None, :]
    imag_freq = frequencies[:, None, None]
    modulus = detuning[None] ** 2 + imag_freq**2
    return (detuning[None] / modulus, -imag_freq / modulus)


def window_sigma(elements, screened, weight_real, weight_imag, band_count):
    row_count = elements.shape[0]
    local_elems = elements.astype(jnp.float32).reshape(row_count, band_count, 2, STATES)
    image_cols = screened.reshape(row_count, band_count, 2, STATES)
    intersection = jnp.einsum(
        "gnpi,gnqj->npiqj", local_elems, image_cols, precision=lax.Precision.HIGHEST
    )
    intersection_real = intersection[:, 0, :, 0, :] + intersection[:, 1, :, 1, :]
    intersection_imag = intersection[:, 0, :, 1, :] - intersection[:, 1, :, 0, :]
    sigma_real = jnp.einsum(
        "kin,nij->kij", weight_real, intersection_real, precision=lax.Precision.HIGHEST
    ) - jnp.einsum("kin,nij->kij", weight_imag, intersection_imag, precision=lax.Precision.HIGHEST)
    sigma_imag = jnp.einsum(
        "kin,nij->kij", weight_real, intersection_imag, precision=lax.Precision.HIGHEST
    ) + jnp.einsum("kin,nij->kij", weight_imag, intersection_real, precision=lax.Precision.HIGHEST)
    return jnp.stack([sigma_real, sigma_imag]) / NG


def shards(pair_elements, screening, energies, frequencies, qp_index, occupied):
    col_count = pair_elements.shape[1]
    band_count = col_count // (2 * STATES)
    gathered = lax.all_gather(pair_elements, "ga", axis=0, tiled=True)
    screened = jnp.dot(
        gathered_by_axis(screening, BLK, (2, 0, 1), 1), gathered, preferred_element_type=jnp.float32
    )
    band_start = lax.axis_index(BLK) * band_count
    weight_real, weight_imag = band_weights(
        energies, frequencies, qp_index, occupied, band_start, band_count
    )
    partial_value = window_sigma(pair_elements, screened, weight_real, weight_imag, band_count)
    return lax.psum(partial_value, BLK_GA)


def solution(mesh):
    torus = Mesh(mesh.devices.reshape(8, 4, 2, mesh.shape["ga"]), ("blk_0", "blk_1", "blk_2", "ga"))
    in_specs = (P("ga", BLK), P("ga", BLK), P(), P(), P(), P())
    out_specs = P()
    return jax.shard_map(
        shards, mesh=torus, in_specs=in_specs, out_specs=out_specs, check_vma=False
    )
```

profile of v0, /device:TPU:23, one launch (start us, length us, event | category | flops | bytes accessed | tf_op | source)
XLA Modules:
  0.0 498.5 jit_solution(6160109027785036022)
XLA Ops:
  6.6 4.7 all-gather
  11.3 0.7 copy.75
  12.0 0.0 all-gather.7.cloned.1.call-start
  12.0 40.0 %all-gather.5.cloned.1.call-done = bf16[16,512,64]{1,2,0:T(8,128)(2,1)} async-done(((bf16[2,512,64]{1,2,0:T(8,128)(2,1)}), bf16[16,512,64]{1,2,0:T(8,128)(2,1)}) %all-gather.5.cloned.1.call-update) | async-done | bytes 1048592 | tf_op jit(solution)/shard_map/all_gather | solution.py:22
  52.1 2.3 copy.61
  54.4 0.0 all-reduce.2.cloned.1.call-start
  54.5 0.1 dynamic_slice.3
  54.6 0.2 select_reduce_fusion
  54.8 0.1 broadcast_subtract_fusion
  54.9 55.8 %all-gather.7.cloned.1.call-done = bf16[64,512,64]{1,2,0:T(8,128)(2,1)} async-done(((bf16[16,512,64]{1,2,0:T(8,128)(2,1)}), bf16[64,512,64]{1,2,0:T(8,128)(2,1)}) %all-gather.7.cloned.1.call-update) | async-done | bytes 4194320 | tf_op jit(solution)/shard_map/all_gather | solution.py:22
  110.7 4.6 copy.60
  115.3 82.6 %all-gather.9.cloned.1.call-done = bf16[4096,1024]{0,1:T(8,128)(2,1)} async-done(((bf16[512,1024]{0,1:T(8,128)(2,1)}), bf16[4096,1024]{0,1:T(8,128)(2,1)}) %all-gather.9.cloned.1.call-update) | async-done | bytes 8388624 | tf_op jit(solution)/shard_map/all_gather | solution.py:67
  197.9 8.2 %fusion.25 = f32[512,16,2,32]{0,3,2,1:T(8,128)S(1)} fusion(bf16[512,4096,1,1]{0,1,3,2:T(8,128)(2,1)} %bitcast.52, bf16[16,2,32,4096]{3,2,1,0:T(8,128)(2,1)} %bitcast.55), kind=kOutput, calls=%fused_computation.35 | convolution fusion | flops 4294967296 | bytes 14680064 | tf_op jit(solution)/shard_map/dot_general | solution.py:68
  206.2 2.7 fusion.2
  208.8 0.1 fusion.8
  208.9 0.2 copy.65
  209.1 0.2 copy.64
  209.3 0.4 fusion.9
  209.7 0.4 fusion.10
  210.1 0.4 fusion.5
  210.5 0.4 fusion.6
  211.0 0.7 maximum_multiply_fusion
  211.7 278.5 %all-reduce.2.cloned.1.call-done = f32[2,8,32,32]{3,1,2,0:T(8,128)} async-done(((f32[2,8,32,32]{3,1,2,0:T(8,128)}), f32[2,8,32,32]{3,1,2,0:T(8,128)}) %all-reduce.2.cloned.1.call-update) | async-done | bytes 65552 | tf_op jit(solution)/shard_map/psum | solution.py:76
  490.3 1.7 copy.68
  (18 shorter events, 0.2 us)
Async XLA Ops:
  6.5 47.9 %copy-start.1 = (f32[1024]{0:T(1024)S(1)}, f32[1024]{0:T(1024)}, u32[]{:S(2)}) copy-start(f32[1024]{0:T(1024)} %param.8) | copy-start | bytes 12292
  6.5 47.9 %copy-start.2 = (s32[1024]{0:T(1024)S(1)}, s32[1024]{0:T(1024)}, u32[]{:S(2)}) copy-start(s32[1024]{0:T(1024)} %param.11) | copy-start | bytes 12292
  6.5 48.0 %copy-start.3 = (s32[32]{0:T(128)S(1)}, s32[32]{0:T(128)}, u32[]{:S(2)}) copy-start(s32[32]{0:T(128)} %param.10) | copy-start | bytes 388
  6.5 48.2 %copy-start.4 = (f32[8]{0:T(128)S(1)}, f32[8]{0:T(128)}, u32[]{:S(2)}) copy-start(f32[8]{0:T(128)} %param.9) | copy-start | bytes 100
  6.5 45.5 %all-gather.5.cloned.1.call-start = ((), (), s32[]{:S(2)}) async-start(), calls=%async_computation | async-start | bytes 1179648 | tf_op jit(solution)/shard_map/all_gather | solution.py:22
  12.0 98.7 %all-gather.7.cloned.1.call-start = ((), (), s32[]{:S(2)}) async-start(), calls=%async_computation.1 | async-start | bytes 5242880 | tf_op jit(solution)/shard_map/all_gather | solution.py:22
  52.1 145.9 %all-gather.9.cloned.1.call-start = ((), (), s32[]{:S(2)}) async-start(), calls=%async_computation.2 | async-start | bytes 9437184 | tf_op jit(solution)/shard_map/all_gather | solution.py:67
  54.4 435.8 %all-reduce.2.cloned.1.call-start = ((), (), s32[]{:S(2)}) async-start(), calls=%async_computation.3 | async-start | bytes 524288 | tf_op jit(solution)/shard_map/psum | solution.py:76
  197.9 8.2 %copy-start = (bf16[512,1024]{0,1:T(8,128)(2,1)S(1)}, bf16[512,1024]{0,1:T(8,128)(2,1)}, u32[]{:S(2)}) copy-start(bf16[512,1024]{0,1:T(8,128)(2,1)} %copy.61) | copy-start | bytes 3145732
Sparse Core Ops, SparseCore 0:
  12.1 39.9 all-gather.4
  54.1 56.5 all-gather.6
  112.8 85.0 all-gather.8
  211.8 278.3 all-reduce.1
where the time goes:
time: 499 us; the launch traced here: 498 us
  waiting for transfers between devices  457 us (92%)
  between operations  13.3 us (3%)
  matrix products  12.6 us (3%)
  local copies, waits for them, and re-layouts  9.7 us (2%)
    psum x1, waiting for transfers between devices, shards(): return lax.psum(partial_value, BLK_GA)  279 us
    all_gather x2, waiting for transfers between devices, all_blocks(): pieces = lax.all_gather(pieces, axes[k], axis=0, tiled=True)  95.9 us
    all_gather x1, waiting for transfers between devices, shards(): gathered = lax.all_gather(pair_elements, 'ga', axis=0, tiled=True)  82.6 us
  transfers between devices with their start and end apart: 4, of which 4 were waited for; matrix products, arithmetic and copies ran while one was open for 1% of the time, Pallas kernels for 0%

commit v1 on v0

--- a/solution.py
+++ b/solution.py
@@ -64,7 +64,9 @@
 def shards(pair_elements, screening, energies, frequencies, qp_index, occupied):
     col_count = pair_elements.shape[1]
     band_count = col_count // (2 * STATES)
-    gathered = lax.all_gather(pair_elements, "ga", axis=0, tiled=True)
+    gathered = jnp.concatenate(
+        lax.all_to_all(jnp.stack([pair_elements] * lax.axis_size("ga")), "ga", 0, 0), axis=0
+    )
     screened = jnp.dot(
         gathered_by_axis(screening, BLK, (2, 0, 1), 1), gathered, preferred_element_type=jnp.float32
     )

time: 499 us -> 610 us (1.22)
  blocking collectives: 4.68 us -> 184 us
  waiting for transfers between devices: 457 us -> 368 us
  local copies, waits for them, and re-layouts: 9.7 us -> 20.9 us
  starting transfers between devices: 0.16 us -> 11.2 us
    all_gather x1, blocking collectives: 4.68 us -> 184 us  [all_blocks(): pieces = lax.all_gather(pieces, axes[k], axis=0, tiled=True)]
    all_gather x1 -> x0, waiting for transfers between devices: 82.6 us -> none  [shards(): gathered = lax.all_gather(pair_elements, 'ga', axis=0, tiled=True)]
    all_to_all x0 -> x1, starting transfers between devices: none -> 11.1 us  [shards(): lax.all_to_all(jnp.stack([pair_elements] * lax.axis_size('ga')), 'ga', 0, 0)]
    reshape x0 -> x1, local copies, waits for them, and re-layouts: none -> 8.06 us  [shards(): jnp.concatenate(lax.all_to_all(jnp.stack([pair_elements] * lax.axis_size(...]
  transfers between devices with their start and end apart: 4 -> 4, of which waited for: 4 -> 3; matrix products, arithmetic and copies ran while one was open for 1% -> 1% of each run, Pallas kernels for 0% -> 0%
where the time goes in v1:
time: 610 us
  waiting for transfers between devices  368 us (60%)
  blocking collectives  184 us (30%)
  local copies, waits for them, and re-layouts  20.9 us (3%)
  between operations  13.2 us (2%)
  starting transfers between devices  11.2 us (2%)
  matrix products  11.2 us (2%)
    psum x1, waiting for transfers between devices, shards(): return lax.psum(partial_value, BLK_GA)  275 us
    all_gather x1, blocking collectives, all_blocks(): pieces = lax.all_gather(pieces, axes[k], axis=0, tiled=True)  184 us
    all_gather x2, waiting for transfers between devices, all_blocks(): pieces = lax.all_gather(pieces, axes[k], axis=0, tiled=True)  93.1 us
  transfers between devices with their start and end apart: 4, of which 3 were waited for; matrix products, arithmetic and copies ran while one was open for 1% of the time, Pallas kernels for 0%

profile of v1, /device:TPU:23, one launch (start us, length us, event | category | flops | bytes accessed | tf_op | source)
XLA Modules:
  0.0 609.5 jit_solution(14493006280054148543)
XLA Ops:
  6.5 1.5 copy.63
  8.0 4.0 stack.8
  12.0 11.1 %all-to-all-start = ((bf16[8,512,1024]{1,2,0:T(8,128)(2,1)}), bf16[8,512,1024]{1,2,0:T(8,128)(2,1)}, u32[]{:S(2)}, u32[]{:S(2)}) async-start(bf16[8,512,1024]{1,2,0:T(8,128)(2,1)} %stack.8), calls=%async_computation | async-start | bytes 16777216 | tf_op jit(solution)/shard_map/all_to_all | solution.py:68
  23.1 183.9 %all-gather = bf16[1024,64]{0,1:T(8,128)(2,1)S(1)} all-gather(bf16[512,64]{0,1:T(8,128)(2,1)S(1)} %copy-done.1), channel_id=2, replica_groups=mesh['blk_0'=8,'blk_1'=4,'blk_2'=2,'ga'=8] {'blk_2'}, dimensions={0}, use_global_device_ids=true | all-gather | bytes 196608 | tf_op jit(solution)/shard_map/all_gather | solution.py:22
  207.1 0.7 copy.79
  207.8 34.9 %all-gather.4.cloned.1.call-done = bf16[16,512,64]{1,2,0:T(8,128)(2,1)} async-done(((bf16[2,512,64]{1,2,0:T(8,128)(2,1)}), bf16[16,512,64]{1,2,0:T(8,128)(2,1)}) %all-gather.4.cloned.1.call-update) | async-done | bytes 1048592 | tf_op jit(solution)/shard_map/all_gather | solution.py:22
  242.8 0.1 dynamic_slice.3
  242.9 0.2 select_reduce_fusion
  243.1 0.1 broadcast_subtract_fusion
  243.2 58.2 %all-gather.6.cloned.1.call-done = bf16[64,512,64]{1,2,0:T(8,128)(2,1)} async-done(((bf16[16,512,64]{1,2,0:T(8,128)(2,1)}), bf16[64,512,64]{1,2,0:T(8,128)(2,1)}) %all-gather.6.cloned.1.call-update) | async-done | bytes 4194320 | tf_op jit(solution)/shard_map/all_gather | solution.py:22
  301.4 4.6 copy.62
  306.0 8.1 %copy.77 = bf16[8,128,8,512]{3,2,0,1:T(8,128)(2,1)} copy(bf16[8,128,8,512]{3,2,1,0:T(8,128)(2,1)} %bitcast.32) | data formatting | bytes 16777216 | tf_op jit(solution)/shard_map/reshape | solution.py:67
  314.1 6.9 %fusion.25 = f32[512,16,2,32]{0,3,2,1:T(8,128)S(1)} fusion(bf16[512,4096,1,1]{0,1,3,2:T(8,128)(2,1)S(1)} %bitcast.56, bf16[16,2,32,4096]{3,2,1,0:T(8,128)(2,1)} %bitcast.54), kind=kOutput, calls=%fused_computation.35 | convolution fusion | flops 4294967296 | bytes 14680064 | tf_op jit(solution)/shard_map/dot_general | solution.py:70
  320.9 2.7 fusion.2
  323.7 0.1 fusion.8
  323.7 0.2 copy.67
  323.9 0.2 copy.68
  324.1 0.4 fusion.10
  324.5 0.4 fusion.9
  324.9 0.4 fusion.6
  325.3 0.4 fusion.5
  325.8 0.7 maximum_multiply_fusion
  326.5 274.8 %all-reduce.2.cloned.1.call-done = f32[2,8,32,32]{3,1,2,0:T(8,128)} async-done(((f32[2,8,32,32]{3,1,2,0:T(8,128)}), f32[2,8,32,32]{3,1,2,0:T(8,128)}) %all-reduce.2.cloned.1.call-update) | async-done | bytes 65552 | tf_op jit(solution)/shard_map/psum | solution.py:78
  601.3 1.7 copy.71
  (21 shorter events, 0.2 us)
Async XLA Ops:
  12.0 11.1 %copy-start.1 = (bf16[512,64]{0,1:T(8,128)(2,1)S(1)}, bf16[512,64]{0,1:T(8,128)(2,1)}, u32[]{:S(2)}) copy-start(bf16[512,64]{0,1:T(8,128)(2,1)} %param.7) | copy-start | bytes 196612
  12.0 230.8 %copy-start.2 = (f32[1024]{0:T(1024)S(1)}, f32[1024]{0:T(1024)}, u32[]{:S(2)}) copy-start(f32[1024]{0:T(1024)} %param.8) | copy-start | bytes 12292
  12.0 230.8 %copy-start.3 = (s32[1024]{0:T(1024)S(1)}, s32[1024]{0:T(1024)}, u32[]{:S(2)}) copy-start(s32[1024]{0:T(1024)} %param.11) | copy-start | bytes 12292
  12.0 230.9 %copy-start.4 = (s32[32]{0:T(128)S(1)}, s32[32]{0:T(128)}, u32[]{:S(2)}) copy-start(s32[32]{0:T(128)} %param.10) | copy-start | bytes 388
  12.0 231.1 %copy-start.5 = (f32[8]{0:T(128)S(1)}, f32[8]{0:T(128)}, u32[]{:S(2)}) copy-start(f32[8]{0:T(128)} %param.9) | copy-start | bytes 100
  12.0 294.0 %all-to-all-start = ((bf16[8,512,1024]{1,2,0:T(8,128)(2,1)}), bf16[8,512,1024]{1,2,0:T(8,128)(2,1)}, u32[]{:S(2)}, u32[]{:S(2)}) async-start(bf16[8,512,1024]{1,2,0:T(8,128)(2,1)} %stack.8), calls=%async_computation | async-start | bytes 16777216 | tf_op jit(solution)/shard_map/all_to_all | solution.py:68
  23.1 219.6 %all-gather.4.cloned.1.call-start = ((), (), s32[]{:S(2)}) async-start(), calls=%async_computation.1 | async-start | bytes 1179648 | tf_op jit(solution)/shard_map/all_gather | solution.py:22
  207.8 93.6 %all-gather.6.cloned.1.call-start = ((), (), s32[]{:S(2)}) async-start(), calls=%async_computation.2 | async-start | bytes 5242880 | tf_op jit(solution)/shard_map/all_gather | solution.py:22
  242.7 358.6 %all-reduce.2.cloned.1.call-start = ((), (), s32[]{:S(2)}) async-start(), calls=%async_computation.3 | async-start | bytes 524288 | tf_op jit(solution)/shard_map/psum | solution.py:78
  306.0 8.1 %copy-start = (bf16[8,4,2,512,64]{3,4,2,1,0:T(8,128)(2,1)S(1)}, bf16[8,4,2,512,64]{3,4,2,1,0:T(8,128)(2,1)}, u32[]{:S(2)}) copy-start(bf16[8,4,2,512,64]{3,4,2,1,0:T(8,128)(2,1)} %copy.62) | copy-start | bytes 12582916
Sparse Core Ops, SparseCore 0:
  207.9 34.7 all-gather.3
  244.8 56.5 all-gather.5
  326.6 274.6 all-reduce.1
